TPU v7x, 32 devices: a whole 2x2x4 slice. The times are simulated.
32 devices in a mesh: grp: 2 (over core), tp: 4 (over y, x), src: 4 (over z).
Axes of the slice: x: 2, y: 2, z: 4, core: 2. Of those that a mesh axis runs over, the one named last changes fastest.
Arguments:
- hidden_in: bfloat16 [512, 5120], P(('grp', 'src')), may hold values from -6 to 6
- attn_gain: float32 [5120], replicated, may hold values from 0.5 to 1.5
- w_qkv: int32 [1280, 5120], P(None, 'tp'), may hold values from -2147483648 to 2147483646
- qkv_scale: float32 [5120], P('tp'), may hold values from 0.0001118034 to 0.00041926274
- q_gain: float32 [128], replicated, may hold values from 0.25 to 1.75
- k_gain: float32 [128], replicated, may hold values from 0.1 to 1.9
- key_cache: bfloat16 [8, 64, 128, 512], P(('grp', 'src'), 'tp'), may hold values from -400 to 400
- value_cache: bfloat16 [8, 64, 128, 512], P(('grp', 'src'), 'tp'), may hold values from -9 to 9
- lengths: int32 [8, 64], P(('grp', 'src'), 'tp'), may hold values from 1 to 128, as said below
- w_out: int32 [1024, 5120], P('tp'), may hold values from -2147483648 to 2147483646
- out_scale: float32 [5120], replicated, may hold values from 0.0003125 to 0.00125
- mlp_gain: float32 [5120], replicated, may hold values from 0.5 to 1.5
- w_gate: int32 [1280, 12800], P(('grp', 'src'), 'tp'), may hold values from -2147483648 to 2147483646
- w_up: int32 [1280, 12800], P(('grp', 'src'), 'tp'), may hold values from -2147483648 to 2147483646
- gate_scale: float32 [12800], P('tp'), may hold values from 0.0001118034 to 0.00041926274
- up_scale: float32 [12800], P('tp'), may hold values from 0.0001118034 to 0.00041926274
- w_down: int32 [3200, 5120], P('tp', ('grp', 'src')), may hold values from -2147483648 to 2147483646
- down_scale: float32 [5120], replicated, may hold values from 0.00013258251 to 0.00053033006
Outputs:
- layer_out: bfloat16 [512, 5120], P(('grp', 'src'), 'tp')
Inputs may be any that keep to these rules, and one draw needn't show every extreme that they name: `lengths`: some sequence has exactly 128 cached positions.
All inputs are finite; a program needn't handle non-finite values.
Results may differ from a plain program's by a relative error of at most 0.028.
Values may be sent and summed in bfloat16 or wider, within the bound.
A program may use at most 128 MiB of HBM per device.

v0:
```python
import math
import jax
import jax.numpy as jnp
from jax import lax
from jax.sharding import PartitionSpec as P

D = 5120
QUERY_HEADS = 32
KEY_VALUE_HEADS = 4
HEAD_SIZE = 128
QUERY_COLUMNS = 4096
KEY_COLUMNS = 512
norm_epsilon = 1e-06
rope_base = 1000000.0


def unpack_bytes(packed, byte_index):
    return jnp.right_shift(jnp.left_shift(packed, 24 - 8 * byte_index), 24)


def byte_product(activations, packed):
    products = [
        jnp.dot(
            activations[:, byte_index::4],
            unpack_bytes(packed, byte_index).astype(jnp.bfloat16),
            preferred_element_type=jnp.float32,
        )
        for byte_index in range(4)
    ]
    return products[0] + products[1] + products[2] + products[3]


def normalize_rows(values, gain_row):
    return (
        values
        * lax.rsqrt(jnp.mean(values * values, axis=-1, keepdims=True) + norm_epsilon)
        * gain_row
    )


def rotary_embed(values, positions):
    half_dim = values.shape[-1] // 2
    freq_index = jnp.arange(half_dim, dtype=jnp.float32)
    inverse = jnp.exp(freq_index * (-math.log(rope_base) / half_dim))
    angles = positions.astype(jnp.float32)[:, None] * inverse[None, :]
    cosine = jnp.cos(angles)[:, None, :]
    sine_part = jnp.sin(angles)[:, None, :]
    lower_half = values[..., :half_dim]
    upper_half = values[..., half_dim:]
    return jnp.concatenate(
        [
            lower_half * cosine - upper_half * sine_part,
            upper_half * cosine + lower_half * sine_part,
        ],
        axis=-1,
    )


def local_attention(query_key_value_rows, q_gain, k_gain, stored_keys, stored_values, seq_lengths):
    count_of_rows = query_key_value_rows.shape[0]
    cache_length = stored_keys.shape[1]
    query_matrix = (
        query_key_value_rows[:, :QUERY_COLUMNS]
        .astype(jnp.float32)
        .reshape(count_of_rows, QUERY_HEADS, HEAD_SIZE)
    )
    incoming_keys = (
        query_key_value_rows[:, QUERY_COLUMNS : QUERY_COLUMNS + KEY_COLUMNS]
        .astype(jnp.float32)
        .reshape(count_of_rows, KEY_VALUE_HEADS, HEAD_SIZE)
    )
    incoming_values = query_key_value_rows[:, QUERY_COLUMNS + KEY_COLUMNS :].reshape(
        count_of_rows, KEY_VALUE_HEADS, HEAD_SIZE
    )
    query_matrix = rotary_embed(normalize_rows(query_matrix, q_gain), seq_lengths).astype(
        jnp.bfloat16
    )
    incoming_keys = rotary_embed(normalize_rows(incoming_keys, k_gain), seq_lengths).astype(
        jnp.bfloat16
    )
    query_groups = query_matrix.reshape(
        count_of_rows, KEY_VALUE_HEADS, QUERY_HEADS // KEY_VALUE_HEADS, HEAD_SIZE
    )
    key_slices = stored_keys.reshape(count_of_rows, cache_length, KEY_VALUE_HEADS, HEAD_SIZE)
    value_slices = stored_values.reshape(count_of_rows, cache_length, KEY_VALUE_HEADS, HEAD_SIZE)
    logit_scale = 1.0 / math.sqrt(HEAD_SIZE)
    scores = (
        jnp.einsum("bkgd,bpkd->bkgp", query_groups, key_slices, preferred_element_type=jnp.float32)
        * logit_scale
    )
    live_mask = jnp.arange(cache_length, dtype=jnp.int32)[None, :] < seq_lengths[:, None]
    scores = jnp.where(live_mask[:, None, None, :], scores, -jnp.inf)
    self_score = (
        jnp.einsum("nufi,nui->nuf", query_groups, incoming_keys, preferred_element_type=jnp.float32)
        * logit_scale
    )
    row_max = jnp.maximum(jnp.max(scores, axis=-1), self_score)
    soft_weights = jnp.exp(scores - row_max[..., None])
    own_weight = jnp.exp(self_score - row_max)
    denominator = jnp.sum(soft_weights, axis=-1) + own_weight
    own_low = lax.optimization_barrier(own_weight.astype(jnp.bfloat16)).astype(jnp.float32)
    numerator = jnp.einsum(
        "bkgp,bpkd->bkgd",
        soft_weights.astype(jnp.bfloat16),
        value_slices,
        preferred_element_type=jnp.float32,
    )
    numerator = numerator + own_low[..., None] * incoming_values.astype(jnp.float32)[:, :, None, :]
    return (
        (numerator / denominator[..., None])
        .reshape(count_of_rows, QUERY_COLUMNS)
        .astype(jnp.bfloat16)
    )


def local(
    hidden_in,
    attn_gain,
    w_qkv,
    qkv_scale,
    q_gain,
    k_gain,
    key_cache,
    value_cache,
    lengths,
    w_out,
    out_scale,
    mlp_gain,
    w_gate,
    w_up,
    gate_scale,
    up_scale,
    w_down,
    down_scale,
):
    tp_count = lax.axis_size("tp")
    tp_index = lax.axis_index("tp")
    share_cols = D // tp_count
    residual = hidden_in.astype(jnp.float32)
    normed = normalize_rows(residual, attn_gain).astype(jnp.bfloat16)
    qkv_part = (byte_product(normed, w_qkv) * qkv_scale).astype(jnp.bfloat16)
    query_key_value_rows = lax.all_to_all(qkv_part, "tp", split_axis=0, concat_axis=1, tiled=True)
    heads_out = local_attention(
        query_key_value_rows, q_gain, k_gain, key_cache[0], value_cache[0], lengths[0]
    )
    head_rows = lax.all_to_all(heads_out, "tp", split_axis=1, concat_axis=0, tiled=True)
    partial_value = byte_product(head_rows, w_out) * out_scale
    attn_full = lax.psum(partial_value.astype(jnp.bfloat16), "tp").astype(jnp.float32)
    mid_full = (residual + attn_full).astype(jnp.bfloat16)
    normed_mlp = normalize_rows(mid_full.astype(jnp.float32), mlp_gain).astype(jnp.bfloat16)
    mid_share = lax.dynamic_slice_in_dim(mid_full, tp_index * share_cols, share_cols, 1)
    gate_total = byte_product(
        normed_mlp, lax.all_gather(w_gate, ("grp", "src"), axis=0, tiled=True)
    )
    up_total = byte_product(normed_mlp, lax.all_gather(w_up, ("grp", "src"), axis=0, tiled=True))
    activated = (jax.nn.silu(gate_total * gate_scale) * (up_total * up_scale)).astype(jnp.bfloat16)
    down_terms = (
        byte_product(activated, lax.all_gather(w_down, ("grp", "src"), axis=1, tiled=True))
        * down_scale
    )
    mlp_share = lax.psum_scatter(
        down_terms.astype(jnp.bfloat16), "tp", scatter_dimension=1, tiled=True
    ).astype(jnp.float32)
    return (mid_share.astype(jnp.float32) + mlp_share).astype(jnp.bfloat16)


def solution(mesh):
    return jax.shard_map(
        local,
        mesh=mesh,
        in_specs=(
            P(("grp", "src"), None),
            P(),
            P(None, "tp"),
            P("tp"),
            P(),
            P(),
            P(("grp", "src"), "tp", None, None),
            P(("grp", "src"), "tp", None, None),
            P(("grp", "src"), "tp"),
            P("tp", None),
            P(),
            P(),
            P(("grp", "src"), "tp"),
            P(("grp", "src"), "tp"),
            P("tp"),
            P("tp"),
            P("tp", ("grp", "src")),
            P(),
        ),
        out_specs=P(("grp", "src"), "tp"),
        check_vma=False,
    )
```

profile of v0, /device:TPU:0, one launch (start us, length us, event | category | flops | bytes accessed | tf_op | source)
XLA Modules:
  0.0 582.0 jit_solution(6829318386932394782)
XLA Ops:
  7.4 1.3 fusion.81
  8.7 1.3 fusion.83
  10.0 6.5 %slice.73 = bf16[64,1280]{1,0:T(8,128)(2,1)S(1)} slice(bf16[64,5120]{1,0:T(8,128)(2,1)S(1)} %fusion.83), slice={[0:64:1], [0:5120:4]} | slice | bytes 327680 | tf_op jit(solution)/shard_map/slice | solution.py:24
  16.6 6.6 %slice.74 = bf16[64,1280]{1,0:T(8,128)(2,1)S(1)} slice(bf16[64,5120]{1,0:T(8,128)(2,1)S(1)} %fusion.83), slice={[0:64:1], [1:5120:4]} | slice | bytes 327680 | tf_op jit(solution)/shard_map/slice | solution.py:24
  23.1 6.5 %slice.75 = bf16[64,1280]{1,0:T(8,128)(2,1)S(1)} slice(bf16[64,5120]{1,0:T(8,128)(2,1)S(1)} %fusion.83), slice={[0:64:1], [2:5120:4]} | slice | bytes 327680 | tf_op jit(solution)/shard_map/slice | solution.py:24
  29.6 6.7 %slice.76 = bf16[64,1280]{1,0:T(8,128)(2,1)S(1)} slice(bf16[64,5120]{1,0:T(8,128)(2,1)S(1)} %fusion.83), slice={[0:64:1], [3:5120:4]} | slice | bytes 327680 | tf_op jit(solution)/shard_map/slice | solution.py:24
  36.4 4.0 fusion.50
  40.4 0.7 copy-done.1
  41.1 1.0 fusion.71
  42.2 1.0 fusion.70
  43.2 1.5 fusion.73
  44.8 5.3 all-to-all-start
  50.1 2.6 reshape_squeeze.6
  52.7 4.0 reshape_squeeze.7
  56.7 0.1 multiply_cosine_fusion
  57.1 0.1 multiply_reduce_fusion
  57.4 0.1 multiply_multiply_fusion
  57.5 0.1 subtract_convert_fusion.1
  57.6 0.1 fusion.103
  57.9 0.3 fusion.106
  58.1 1.3 fusion.148
  59.5 0.3 fusion.100
  59.9 2.3 fusion.97
  62.3 9.2 %all_to_all.35 = bf16[16,4,1024]{2,0,1:T(8,128)(2,1)S(1)} all-to-all(bf16[16,4,1024]{2,0,1:T(8,128)(2,1)S(1)} %copy.28), channel_id=1, replica_groups=mesh['grp'=2,'tp'=4,'src'=4] {'tp'}, dimensions={1} | all-to-all | bytes 262144 | tf_op jit(solution)/shard_map/all_to_all | solution.py:146
  71.5 1.1 slice.84
  72.7 1.1 slice.85
  73.8 1.1 slice.86
  75.0 1.1 slice.87
  76.1 3.5 fusion.61
  79.6 3.5 convolution_add_fusion.2
  83.1 0.9 convolution_add_fusion.1
  84.0 1.6 fusion.39
  85.7 0.5 all-gather.4.cloned.1.call-update
  86.3 0.5 all-gather.6.cloned.1.call-update
  86.9 0.5 all-gather.8.cloned.1.call-update
  87.5 44.9 %all-reduce.2.cloned.1.call-done = bf16[64,5120]{1,0:T(8,128)(2,1)} async-done(((bf16[64,5120]{1,0:T(8,128)(2,1)}), bf16[64,5120]{1,0:T(8,128)(2,1)}) %all-reduce.2.cloned.1.call-update) | async-done | bytes 655376 | tf_op jit(solution)/shard_map/psum | solution.py:148
  132.4 1.4 fusion.78
  133.8 0.2 fusion.80
  134.0 7.0 %slice.88 = bf16[64,1280]{1,0:T(8,128)(2,1)S(1)} slice(bf16[64,5120]{1,0:T(8,128)(2,1)S(1)} %fusion.80), slice={[0:64:1], [0:5120:4]} | slice | bytes 327680 | tf_op jit(solution)/shard_map/slice | solution.py:24
  141.0 6.6 %slice.89 = bf16[64,1280]{1,0:T(8,128)(2,1)S(1)} slice(bf16[64,5120]{1,0:T(8,128)(2,1)S(1)} %fusion.80), slice={[0:64:1], [1:5120:4]} | slice | bytes 327680 | tf_op jit(solution)/shard_map/slice | solution.py:24
  147.6 6.5 %slice.90 = bf16[64,1280]{1,0:T(8,128)(2,1)S(1)} slice(bf16[64,5120]{1,0:T(8,128)(2,1)S(1)} %fusion.80), slice={[0:64:1], [2:5120:4]} | slice | bytes 327680 | tf_op jit(solution)/shard_map/slice | solution.py:24
  154.1 6.7 %slice.91 = bf16[64,1280]{1,0:T(8,128)(2,1)S(1)} slice(bf16[64,5120]{1,0:T(8,128)(2,1)S(1)} %fusion.80), slice={[0:64:1], [3:5120:4]} | slice | bytes 327680 | tf_op jit(solution)/shard_map/slice | solution.py:24
  160.8 74.5 %all-gather.4.cloned.1.call-done = s32[1280,3200]{1,0:T(8,128)} async-done(((s32[160,3200]{1,0:T(8,128)}), s32[1280,3200]{1,0:T(8,128)}) %all-gather.4.cloned.1.call-update) | async-done | bytes 16384016 | tf_op jit(solution)/shard_map/all_gather | solution.py:153
  235.3 8.0 %fusion = f32[64,3200]{1,0:T(8,128)S(1)} fusion(bf16[64,1280]{1,0:T(8,128)(2,1)S(1)} %slice.88, s32[1280,3200]{1,0:T(8,128)} %all-gather.4.cloned.1.call-done), kind=kOutput, calls=%fused_computation.12 | convolution fusion | flops 536576000 | bytes 17367040 | tf_op jit(solution)/shard_map/dot_general | solution.py:23
  243.3 139.4 %all-gather.6.cloned.1.call-done = s32[1280,3200]{1,0:T(8,128)} async-done(((s32[160,3200]{1,0:T(8,128)}), s32[1280,3200]{1,0:T(8,128)}) %all-gather.6.cloned.1.call-update) | async-done | bytes 16384016 | tf_op jit(solution)/shard_map/all_gather | solution.py:155
  382.7 8.1 %fusion.4 = f32[64,3200]{1,0:T(8,128)S(1)} fusion(bf16[64,1280]{1,0:T(8,128)(2,1)S(1)} %slice.88, s32[1280,3200]{1,0:T(8,128)} %all-gather.6.cloned.1.call-done), kind=kOutput, calls=%fused_computation.16 | convolution fusion | flops 536576000 | bytes 17367040 | tf_op jit(solution)/shard_map/dot_general | solution.py:23
  390.8 9.9 %fusion.45 = f32[64,3200]{1,0:T(8,128)S(1)} fusion(f32[64,3200]{1,0:T(8,128)S(1)} %fusion, bf16[64,1280]{1,0:T(8,128)(2,1)S(1)} %slice.89, s32[1280,3200]{1,0:T(8,128)} %all-gather.4.cloned.1.call-done), kind=kOutput, calls=%fused_computation.68 | convolution fusion | flops 536780800 | bytes 18186240 | tf_op jit(solution)/shard_map/dot_general | solution.py:23
  400.8 2.4 fusion.42
  403.2 8.0 %fusion.44 = f32[64,3200]{1,0:T(8,128)S(1)} fusion(f32[64,3200]{1,0:T(8,128)S(1)} %fusion.45, bf16[64,1280]{1,0:T(8,128)(2,1)S(1)} %slice.90, s32[1280,3200]{1,0:T(8,128)} %all-gather.4.cloned.1.call-done), kind=kOutput, calls=%fused_computation.67 | convolution fusion | flops 536780800 | bytes 18186240 | tf_op jit(solution)/shard_map/dot_general | solution.py:23
  411.2 2.6 fusion.41
  413.9 7.6 %fusion.46 = f32[64,3200]{1,0:T(8,128)S(1)} fusion(f32[64,3200]{1,0:T(8,128)S(1)} %fusion.44, bf16[64,1280]{1,0:T(8,128)(2,1)S(1)} %slice.91, s32[1280,3200]{1,0:T(8,128)} %all-gather.4.cloned.1.call-done, f32[3200]{0:T(1024)S(1)} %copy-done.7), kind=kOutput, calls=%fused_computation.69 | convolution fusion | flops 536985600 | bytes 18199040 | tf_op jit(solution)/shard_map/dot_general | solution.py:23
  421.5 2.0 fusion.49
  423.5 3.7 slice.92
  427.2 3.7 slice.93
  430.9 3.7 slice.94
  434.6 4.0 slice.95
  438.6 91.5 %all-gather.8.cloned.1.call-done = s32[800,5120]{1,0:T(8,128)} async-done(((s32[800,640]{1,0:T(8,128)}), s32[800,5120]{1,0:T(8,128)}) %all-gather.8.cloned.1.call-update) | async-done | bytes 16384016 | tf_op jit(solution)/shard_map/all_gather | solution.py:158
  530.1 8.2 %fusion.8 = f32[64,5120]{1,0:T(8,128)S(1)} fusion(bf16[64,800]{1,0:T(8,128)(2,1)S(1)} %slice.92, s32[800,5120]{1,0:T(8,128)} %all-gather.8.cloned.1.call-done), kind=kOutput, calls=%fused_computation.20 | convolution fusion | flops 536576000 | bytes 17797120 | tf_op jit(solution)/shard_map/dot_general | solution.py:23
  538.3 2.1 copy-done
  540.4 2.5 fusion.36
  542.9 2.5 fusion.35
  545.4 2.9 fusion.38
  548.3 24.0 %reduce-scatter.2.cloned.1.call-done = bf16[64,1280]{1,0:T(8,128)(2,1)} async-done(((bf16[64,5120]{1,0:T(8,128)(2,1)}), bf16[64,1280]{1,0:T(8,128)(2,1)}) %reduce-scatter.2.cloned.1.call-update) | async-done | bytes 163856 | tf_op jit(solution)/shard_map/reduce_scatter | solution.py:161
  572.3 1.6 add_convert_fusion
  (65 shorter events, 0.9 us)
Async XLA Ops:
  36.4 4.7 copy-start.1
  41.1 2.1 copy-start.8
  42.2 8.0 %copy-start.11 = (s32[1,16]{1,0:T(1,128)S(1)}, s32[1,16]{1,0:T(1,128)}, u32[]{:S(2)}) copy-start(s32[1,16]{1,0:T(1,128)} %param.26) | copy-start | bytes 196
  44.8 12.5 %copy-start.9 = (f32[128]{0:T(128)S(1)}, f32[128]{0:T(128)}, u32[]{:S(2)}) copy-start(f32[128]{0:T(128)} %param.23) | copy-start | bytes 1540
  44.8 12.6 %copy-start.10 = (f32[128]{0:T(128)S(1)}, f32[128]{0:T(128)}, u32[]{:S(2)}) copy-start(f32[128]{0:T(128)} %param.22) | copy-start | bytes 1540
  44.8 12.1 %all-to-all-start = ((bf16[4,16,1280]{2,1,0:T(8,128)(2,1)}), bf16[4,16,1280]{2,1,0:T(8,128)(2,1)S(1)}, u32[]{:S(2)}, u32[]{:S(2)}) async-start(bf16[4,16,1280]{2,1,0:T(8,128)(2,1)} %bitcast.1), calls=%async_computation | async-start | bytes 327680 | tf_op jit(solution)/shard_map/all_to_all | solution.py:142
  50.1 82.3 %all-reduce.2.cloned.1.call-start = ((), (), s32[]{:S(2)}) async-start(), calls=%async_computation.3 | async-start | bytes 1310720 | tf_op jit(solution)/shard_map/psum | solution.py:148
  76.1 7.0 %slice-start.4 = ((s8[5242880]{0:T(1024)(128)(4,1)}), s8[4194304]{0:T(1024)(128)(4,1)S(1)}, s32[]{:S(2)}) async-start(s8[5242880]{0:T(1024)(128)(4,1)} %bitcast.49), calls=%async_computation.12 | async-start | bytes 8388608
  79.6 3.5 slice-start.5
  79.6 4.4 copy-start.4
  84.0 48.3 %copy-start.2 = (bf16[64,5120]{1,0:T(8,128)(2,1)S(1)}, bf16[64,5120]{1,0:T(8,128)(2,1)}, u32[]{:S(2)}) copy-start(bf16[64,5120]{1,0:T(8,128)(2,1)} %param.18) | copy-start | bytes 1966084
  84.0 49.8 %copy-start.5 = (f32[5120]{0:T(1024)S(1)}, f32[5120]{0:T(1024)}, u32[]{:S(2)}) copy-start(f32[5120]{0:T(1024)} %param.29) | copy-start | bytes 61444
  85.7 149.6 %all-gather.4.cloned.1.call-start = ((), (), s32[]{:S(2)}) async-start(), calls=%async_computation.4 | async-start | bytes 18432000 | tf_op jit(solution)/shard_map/all_gather | solution.py:153
  86.3 296.4 %all-gather.6.cloned.1.call-start = ((), (), s32[]{:S(2)}) async-start(), calls=%async_computation.5 | async-start | bytes 18432000 | tf_op jit(solution)/shard_map/all_gather | solution.py:155
  86.9 443.2 %all-gather.8.cloned.1.call-start = ((), (), s32[]{:S(2)}) async-start(), calls=%async_computation.6 | async-start | bytes 18432000 | tf_op jit(solution)/shard_map/all_gather | solution.py:158
  87.4 484.9 %reduce-scatter.2.cloned.1.call-start = ((), (), s32[]{:S(2)}) async-start(), calls=%async_computation.7 | async-start | bytes 819200 | tf_op jit(solution)/shard_map/reduce_scatter | solution.py:161
  382.7 18.1 %slice-start = ((s8[16384000]{0:T(1024)(128)(4,1)}), s8[4194304]{0:T(1024)(128)(4,1)S(1)}, s32[]{:S(2)}) async-start(s8[16384000]{0:T(1024)(128)(4,1)} %bitcast.47), calls=%async_computation.8 | async-start | bytes 8388608
  382.7 18.1 %slice-start.1 = ((s8[16384000]{0:T(1024)(128)(4,1)}), s8[4194304]{0:T(1024)(128)(4,1)S(1)}, s32[]{:S(2)}) async-start(s8[16384000]{0:T(1024)(128)(4,1)} %bitcast.47), calls=%async_computation.9 | async-start | bytes 8388608
  390.8 9.9 %slice-start.2 = ((s8[16384000]{0:T(1024)(128)(4,1)}), s8[4194304]{0:T(1024)(128)(4,1)S(1)}, s32[]{:S(2)}) async-start(s8[16384000]{0:T(1024)(128)(4,1)} %bitcast.47), calls=%async_computation.10 | async-start | bytes 8388608
  390.8 9.9 %slice-start.3 = ((s8[16384000]{0:T(1024)(128)(4,1)}), s8[3801088]{0:T(1024)(128)(4,1)S(1)}, s32[]{:S(2)}) async-start(s8[16384000]{0:T(1024)(128)(4,1)} %bitcast.47), calls=%async_computation.11 | async-start | bytes 7602176
  411.2 2.6 copy-start.7
  413.9 7.6 %copy-start.6 = (f32[3200]{0:T(1024)S(1)}, f32[3200]{0:T(1024)}, u32[]{:S(2)}) copy-start(f32[3200]{0:T(1024)} %param.33) | copy-start | bytes 38404
  530.1 10.3 %copy-start = (s32[800,5120]{1,0:T(8,128)S(1)}, s32[800,5120]{1,0:T(8,128)}, u32[]{:S(2)}) copy-start(s32[800,5120]{1,0:T(8,128)} %all-gather.8.cloned.1.call-done) | copy-start | bytes 49152004
  542.9 2.5 copy-start.3
Sparse Core Ops, SparseCore 0:
  85.8 46.4 all-reduce.1
  548.4 23.8 reduce-scatter.1
Sparse Core Ops, SparseCore 1:
  87.8 147.4 all-gather.3
  236.7 145.9 all-gather.5
  384.2 145.9 all-gather.7
where the time goes:
time: 589 us; the launch traced here: 582 us
  waiting for transfers between devices  376 us (64%)
  matrix products  85.7 us (15%)
  local copies, waits for them, and re-layouts  82.3 us (14%)
  between operations  16.1 us (3%)
  blocking collectives  9.25 us (2%)
  other arithmetic  7.26 us (1%)
    all_gather x1, waiting for transfers between devices, local(): lax.all_gather(w_up, ('grp', 'src'), axis=0, tiled=True)  139 us
    all_gather x1, waiting for transfers between devices, local(): lax.all_gather(w_down, ('grp', 'src'), axis=1, tiled=True)  91.5 us
    dot_general x20, matrix products, byte_product(): jnp.dot(activations[:, byte_index::4], unpack_bytes(packed, byte_index).a...  81.8 us
    all_gather x1, waiting for transfers between devices, local(): lax.all_gather(w_gate, ('grp', 'src'), axis=0, tiled=True)  74.5 us
    slice x16, local copies, waits for them, and re-layouts, byte_product(): activations[:, byte_index::4]  72.7 us
    psum x1, waiting for transfers between devices, local(): lax.psum(partial_value.astype(jnp.bfloat16), 'tp').astype(jnp.float32)  44.9 us
    reduce_scatter x1, waiting for transfers between devices, local(): lax.psum_scatter(down_terms.astype(jnp.bfloat16), 'tp', scatter_dimension...  24 us
  transfers between devices with their start and end apart: 6, of which 5 were waited for; matrix products, arithmetic and copies ran while one was open for 17% of the time, Pallas kernels for 0%

commit v1 on v0

--- a/solution.py
+++ b/solution.py
@@ -12,6 +12,12 @@
 KEY_COLUMNS = 512
 norm_epsilon = 1e-06
 rope_base = 1000000.0
+
+
+def see_frame(unit, net_axis):
+    fresh = lax.all_gather(unit, net_axis)
+    w1 = jnp.concatenate(fresh, axis=1)
+    return w1
 
 
 def unpack_bytes(packed, byte_index):
@@ -154,10 +160,7 @@
     )
     up_total = byte_product(normed_mlp, lax.all_gather(w_up, ("grp", "src"), axis=0, tiled=True))
     activated = (jax.nn.silu(gate_total * gate_scale) * (up_total * up_scale)).astype(jnp.bfloat16)
-    down_terms = (
-        byte_product(activated, lax.all_gather(w_down, ("grp", "src"), axis=1, tiled=True))
-        * down_scale
-    )
+    down_terms = byte_product(activated, see_frame(w_down, net_axis=("grp", "src"))) * down_scale
     mlp_share = lax.psum_scatter(
         down_terms.astype(jnp.bfloat16), "tp", scatter_dimension=1, tiled=True
     ).astype(jnp.float32)

time: 589 us -> 626 us (1.063)
  local copies, waits for them, and re-layouts: 82.3 us -> 109 us
  other arithmetic: 7.26 us -> 24.4 us
    unnamed x37 -> x51, local copies, waits for them, and re-layouts: 2.96 us -> 28 us
    convert_element_type x0 -> x1, other arithmetic: none -> 17 us  [byte_product(): unpack_bytes(packed, byte_index).astype(jnp.bfloat16)]
  transfers between devices with their start and end apart: 6 -> 6, of which waited for: 5 -> 5; matrix products, arithmetic and copies ran while one was open for 17% -> 16% of each run, Pallas kernels for 0% -> 0%
where the time goes in v1:
time: 626 us; the launch traced here: 619 us
  waiting for transfers between devices  374 us (60%)
  local copies, waits for them, and re-layouts  109 us (17%)
  matrix products  80.9 us (13%)
  other arithmetic  24.4 us (4%)
  between operations  16.1 us (3%)
  blocking collectives  9.25 us (1%)
    all_gather x1, waiting for transfers between devices, local(): lax.all_gather(w_up, ('grp', 'src'), axis=0, tiled=True)  139 us
    all_gather x1, waiting for transfers between devices, see_frame(): fresh = lax.all_gather(unit, net_axis)  90.1 us
    dot_general x20, matrix products, byte_product(): jnp.dot(activations[:, byte_index::4], unpack_bytes(packed, byte_index).a...  77 us
    slice x16, local copies, waits for them, and re-layouts, byte_product(): activations[:, byte_index::4]  74.2 us
    all_gather x1, waiting for transfers between devices, local(): lax.all_gather(w_gate, ('grp', 'src'), axis=0, tiled=True)  73.6 us
    psum x1, waiting for transfers between devices, local(): lax.psum(partial_value.astype(jnp.bfloat16), 'tp').astype(jnp.float32)  44.9 us
    unnamed x51, local copies, waits for them, and re-layouts  28 us
    reduce_scatter x1, waiting for transfers between devices, local(): lax.psum_scatter(down_terms.astype(jnp.bfloat16), 'tp', scatter_dimension...  24 us
  transfers between devices with their start and end apart: 6, of which 5 were waited for; matrix products, arithmetic and copies ran while one was open for 16% of the time, Pallas kernels for 0%

profile of v1, /device:TPU:0, one launch (start us, length us, event | category | flops | bytes accessed | tf_op | source)
XLA Modules:
  0.0 618.5 jit_solution(15865815261883425891)
XLA Ops:
  7.4 1.3 fusion.67
  8.7 1.3 fusion.69
  10.0 6.5 %slice.73 = bf16[64,1280]{1,0:T(8,128)(2,1)S(1)} slice(bf16[64,5120]{1,0:T(8,128)(2,1)S(1)} %fusion.69), slice={[0:64:1], [0:5120:4]} | slice | bytes 327680 | tf_op jit(solution)/shard_map/slice | solution.py:30
  16.6 6.6 %slice.74 = bf16[64,1280]{1,0:T(8,128)(2,1)S(1)} slice(bf16[64,5120]{1,0:T(8,128)(2,1)S(1)} %fusion.69), slice={[0:64:1], [1:5120:4]} | slice | bytes 327680 | tf_op jit(solution)/shard_map/slice | solution.py:30
  23.1 6.5 %slice.75 = bf16[64,1280]{1,0:T(8,128)(2,1)S(1)} slice(bf16[64,5120]{1,0:T(8,128)(2,1)S(1)} %fusion.69), slice={[0:64:1], [2:5120:4]} | slice | bytes 327680 | tf_op jit(solution)/shard_map/slice | solution.py:30
  29.6 6.7 %slice.76 = bf16[64,1280]{1,0:T(8,128)(2,1)S(1)} slice(bf16[64,5120]{1,0:T(8,128)(2,1)S(1)} %fusion.69), slice={[0:64:1], [3:5120:4]} | slice | bytes 327680 | tf_op jit(solution)/shard_map/slice | solution.py:30
  36.4 4.0 fusion.36
  40.4 0.7 copy-done
  41.1 1.0 fusion.57
  42.2 1.0 fusion.56
  43.2 1.5 fusion.59
  44.8 5.3 all-to-all-start
  50.1 2.6 reshape_squeeze.6
  52.7 4.0 reshape_squeeze.7
  58.1 1.3 fusion.127
  59.5 0.3 fusion.86
  59.9 2.3 fusion.83
  62.3 9.2 %all_to_all.35 = bf16[16,4,1024]{2,0,1:T(8,128)(2,1)S(1)} all-to-all(bf16[16,4,1024]{2,0,1:T(8,128)(2,1)S(1)} %copy.32), channel_id=1, replica_groups=mesh['grp'=2,'tp'=4,'src'=4] {'tp'}, dimensions={1} | all-to-all | bytes 262144 | tf_op jit(solution)/shard_map/all_to_all | solution.py:152
  71.5 1.1 slice.84
  72.7 1.1 slice.85
  73.8 1.1 slice.86
  75.0 1.1 slice.87
  76.1 3.5 fusion.47
  79.6 3.5 convolution_add_fusion.2
  83.1 0.9 convolution_add_fusion.1
  84.0 1.6 fusion.25
  85.7 0.5 all-gather.5.cloned.1.call-update
  86.3 0.5 all-gather.7.cloned.1.call-update
  86.9 0.5 all-gather.9.cloned.1.call-update
  87.5 44.9 %all-reduce.2.cloned.1.call-done = bf16[64,5120]{1,0:T(8,128)(2,1)} async-done(((bf16[64,5120]{1,0:T(8,128)(2,1)}), bf16[64,5120]{1,0:T(8,128)(2,1)}) %all-reduce.2.cloned.1.call-update) | async-done | bytes 655376 | tf_op jit(solution)/shard_map/psum | solution.py:154
  132.3 1.4 fusion.64
  133.8 0.8 copy-done.3
  134.9 7.0 %slice.88 = bf16[64,1280]{1,0:T(8,128)(2,1)S(1)} slice(bf16[64,5120]{1,0:T(8,128)(2,1)S(1)} %fusion.66), slice={[0:64:1], [0:5120:4]} | slice | bytes 327680 | tf_op jit(solution)/shard_map/slice | solution.py:30
  141.9 6.6 %slice.89 = bf16[64,1280]{1,0:T(8,128)(2,1)S(1)} slice(bf16[64,5120]{1,0:T(8,128)(2,1)S(1)} %fusion.66), slice={[0:64:1], [1:5120:4]} | slice | bytes 327680 | tf_op jit(solution)/shard_map/slice | solution.py:30
  148.4 6.5 %slice.90 = bf16[64,1280]{1,0:T(8,128)(2,1)S(1)} slice(bf16[64,5120]{1,0:T(8,128)(2,1)S(1)} %fusion.66), slice={[0:64:1], [2:5120:4]} | slice | bytes 327680 | tf_op jit(solution)/shard_map/slice | solution.py:30
  154.9 6.7 %slice.91 = bf16[64,1280]{1,0:T(8,128)(2,1)S(1)} slice(bf16[64,5120]{1,0:T(8,128)(2,1)S(1)} %fusion.66), slice={[0:64:1], [3:5120:4]} | slice | bytes 327680 | tf_op jit(solution)/shard_map/slice | solution.py:30
  161.6 73.6 %all-gather.5.cloned.1.call-done = s32[1280,3200]{1,0:T(8,128)} async-done(((s32[160,3200]{1,0:T(8,128)}), s32[1280,3200]{1,0:T(8,128)}) %all-gather.5.cloned.1.call-update) | async-done | bytes 16384016 | tf_op jit(solution)/shard_map/all_gather | solution.py:159
  235.3 8.0 %fusion = f32[64,3200]{1,0:T(8,128)S(1)} fusion(bf16[64,1280]{1,0:T(8,128)(2,1)S(1)} %slice.88, s32[1280,3200]{1,0:T(8,128)} %all-gather.5.cloned.1.call-done), kind=kOutput, calls=%fused_computation.12 | convolution fusion | flops 536576000 | bytes 17367040 | tf_op jit(solution)/shard_map/dot_general | solution.py:29
  243.3 139.4 %all-gather.7.cloned.1.call-done = s32[1280,3200]{1,0:T(8,128)} async-done(((s32[160,3200]{1,0:T(8,128)}), s32[1280,3200]{1,0:T(8,128)}) %all-gather.7.cloned.1.call-update) | async-done | bytes 16384016 | tf_op jit(solution)/shard_map/all_gather | solution.py:161
  382.7 8.1 %fusion.4 = f32[64,3200]{1,0:T(8,128)S(1)} fusion(bf16[64,1280]{1,0:T(8,128)(2,1)S(1)} %slice.88, s32[1280,3200]{1,0:T(8,128)} %all-gather.7.cloned.1.call-done), kind=kOutput, calls=%fused_computation.16 | convolution fusion | flops 536576000 | bytes 17367040 | tf_op jit(solution)/shard_map/dot_general | solution.py:29
  390.8 9.9 %fusion.31 = f32[64,3200]{1,0:T(8,128)S(1)} fusion(f32[64,3200]{1,0:T(8,128)S(1)} %fusion, bf16[64,1280]{1,0:T(8,128)(2,1)S(1)} %slice.89, s32[1280,3200]{1,0:T(8,128)} %all-gather.5.cloned.1.call-done), kind=kOutput, calls=%fused_computation.57 | convolution fusion | flops 536780800 | bytes 18186240 | tf_op jit(solution)/shard_map/dot_general | solution.py:29
  400.8 2.4 fusion.28
  403.2 8.1 %fusion.30 = f32[64,3200]{1,0:T(8,128)S(1)} fusion(f32[64,3200]{1,0:T(8,128)S(1)} %fusion.31, bf16[64,1280]{1,0:T(8,128)(2,1)S(1)} %slice.90, s32[1280,3200]{1,0:T(8,128)} %all-gather.5.cloned.1.call-done), kind=kOutput, calls=%fused_computation.56 | convolution fusion | flops 536780800 | bytes 18186240 | tf_op jit(solution)/shard_map/dot_general | solution.py:29
  411.2 2.6 fusion.27
  413.9 7.6 %fusion.32 = f32[64,3200]{1,0:T(8,128)S(1)} fusion(f32[64,3200]{1,0:T(8,128)S(1)} %fusion.30, bf16[64,1280]{1,0:T(8,128)(2,1)S(1)} %slice.91, s32[1280,3200]{1,0:T(8,128)} %all-gather.5.cloned.1.call-done, f32[3200]{0:T(1024)S(1)} %copy-done.10), kind=kOutput, calls=%fused_computation.58 | convolution fusion | flops 536985600 | bytes 18199040 | tf_op jit(solution)/shard_map/dot_general | solution.py:29
  421.4 2.0 fusion.35
  423.5 4.3 slice.92
  427.8 4.3 slice.93
  432.1 4.3 slice.94
  436.3 3.7 slice.95
  440.0 90.1 %all-gather.9.cloned.1.call-done = s32[6400,640]{1,0:T(8,128)} async-done(((s32[800,640]{1,0:T(8,128)}), s32[6400,640]{1,0:T(8,128)}) %all-gather.9.cloned.1.call-update) | async-done | bytes 16384016 | tf_op jit(solution)/shard_map/all_gather | solution.py:18
  530.1 17.0 %shift-right-arithmetic_convert_fusion = (bf16[6400,640]{1,0:T(8,128)(2,1)}, bf16[6400,640]{1,0:T(8,128)(2,1)S(1)}, bf16[6400,640]{1,0:T(8,128)(2,1)}, bf16[6400,640]{1,0:T(8,128)(2,1)}) fusion(s32[6400,640]{1,0:T(8,128)} %all-gather.9.cloned.1.call-done), kind=kLoop, calls=%fused_computation | loop fusion | flops 49152000 | bytes 49152000 | tf_op jit(solution)/shard_map/convert_element_type | solution.py:31
  547.1 7.9 %copy.41 = bf16[100,8,8,640]{3,1,2,0:T(8,128)(2,1)} copy(bf16[100,8,8,640]{3,1,0,2:T(8,128)(2,1)} %bitcast.88) | data formatting | bytes 16384000
  555.0 7.9 %copy.42 = bf16[100,8,8,640]{3,1,2,0:T(8,128)(2,1)} copy(bf16[100,8,8,640]{3,1,0,2:T(8,128)(2,1)} %bitcast.87) | data formatting | bytes 16384000
  562.9 4.5 copy.43
  567.4 4.7 copy.44
  572.1 5.3 fusion.128
  577.4 0.4 copy-done.1
  577.8 1.7 convolution_add_fusion.5
  579.6 0.9 slice-done.7
  580.4 1.7 convolution_add_fusion.4
  582.2 2.6 fusion.24
  584.8 24.0 %reduce-scatter.2.cloned.1.call-done = bf16[64,1280]{1,0:T(8,128)(2,1)} async-done(((bf16[64,5120]{1,0:T(8,128)(2,1)}), bf16[64,1280]{1,0:T(8,128)(2,1)}) %reduce-scatter.2.cloned.1.call-update) | async-done | bytes 163856 | tf_op jit(solution)/shard_map/reduce_scatter | solution.py:164
  608.8 1.7 add_convert_fusion
  (81 shorter events, 2.1 us)
Async XLA Ops:
  36.4 4.7 copy-start
  41.1 2.1 copy-start.11
  42.2 8.0 %copy-start.14 = (s32[1,16]{1,0:T(1,128)S(1)}, s32[1,16]{1,0:T(1,128)}, u32[]{:S(2)}) copy-start(s32[1,16]{1,0:T(1,128)} %param.26) | copy-start | bytes 196
  44.8 12.5 %copy-start.12 = (f32[128]{0:T(128)S(1)}, f32[128]{0:T(128)}, u32[]{:S(2)}) copy-start(f32[128]{0:T(128)} %param.23) | copy-start | bytes 1540
  44.8 12.6 %copy-start.13 = (f32[128]{0:T(128)S(1)}, f32[128]{0:T(128)}, u32[]{:S(2)}) copy-start(f32[128]{0:T(128)} %param.22) | copy-start | bytes 1540
  44.8 12.1 %all-to-all-start = ((bf16[4,16,1280]{2,1,0:T(8,128)(2,1)}), bf16[4,16,1280]{2,1,0:T(8,128)(2,1)S(1)}, u32[]{:S(2)}, u32[]{:S(2)}) async-start(bf16[4,16,1280]{2,1,0:T(8,128)(2,1)} %bitcast.1), calls=%async_computation | async-start | bytes 327680 | tf_op jit(solution)/shard_map/all_to_all | solution.py:148
  50.1 82.2 %all-reduce.2.cloned.1.call-start = ((), (), s32[]{:S(2)}) async-start(), calls=%async_computation.3 | async-start | bytes 1310720 | tf_op jit(solution)/shard_map/psum | solution.py:154
  76.1 7.0 %slice-start.4 = ((s8[5242880]{0:T(1024)(128)(4,1)}), s8[4194304]{0:T(1024)(128)(4,1)S(1)}, s32[]{:S(2)}) async-start(s8[5242880]{0:T(1024)(128)(4,1)} %bitcast.77), calls=%async_computation.12 | async-start | bytes 8388608
  79.6 3.5 slice-start.5
  79.6 4.4 copy-start.7
  84.0 48.3 %copy-start.2 = (bf16[64,5120]{1,0:T(8,128)(2,1)S(1)}, bf16[64,5120]{1,0:T(8,128)(2,1)}, u32[]{:S(2)}) copy-start(bf16[64,5120]{1,0:T(8,128)(2,1)} %param.18) | copy-start | bytes 1966084
  84.0 50.6 %copy-start.8 = (f32[5120]{0:T(1024)S(1)}, f32[5120]{0:T(1024)}, u32[]{:S(2)}) copy-start(f32[5120]{0:T(1024)} %param.29) | copy-start | bytes 61444
  85.7 149.6 %all-gather.5.cloned.1.call-start = ((), (), s32[]{:S(2)}) async-start(), calls=%async_computation.4 | async-start | bytes 18432000 | tf_op jit(solution)/shard_map/all_gather | solution.py:159
  86.3 296.4 %all-gather.7.cloned.1.call-start = ((), (), s32[]{:S(2)}) async-start(), calls=%async_computation.5 | async-start | bytes 18432000 | tf_op jit(solution)/shard_map/all_gather | solution.py:161
  86.8 443.2 %all-gather.9.cloned.1.call-start = ((), (), s32[]{:S(2)}) async-start(), calls=%async_computation.7 | async-start | bytes 18432000 | tf_op jit(solution)/shard_map/all_gather | solution.py:18
  87.4 521.4 %reduce-scatter.2.cloned.1.call-start = ((), (), s32[]{:S(2)}) async-start(), calls=%async_computation.6 | async-start | bytes 819200 | tf_op jit(solution)/shard_map/reduce_scatter | solution.py:164
  133.8 0.9 copy-start.3
  382.7 18.1 %slice-start = ((s8[16384000]{0:T(1024)(128)(4,1)}), s8[4194304]{0:T(1024)(128)(4,1)S(1)}, s32[]{:S(2)}) async-start(s8[16384000]{0:T(1024)(128)(4,1)} %bitcast.75), calls=%async_computation.8 | async-start | bytes 8388608
  382.7 18.1 %slice-start.1 = ((s8[16384000]{0:T(1024)(128)(4,1)}), s8[4194304]{0:T(1024)(128)(4,1)S(1)}, s32[]{:S(2)}) async-start(s8[16384000]{0:T(1024)(128)(4,1)} %bitcast.75), calls=%async_computation.9 | async-start | bytes 8388608
  390.8 9.9 %slice-start.2 = ((s8[16384000]{0:T(1024)(128)(4,1)}), s8[4194304]{0:T(1024)(128)(4,1)S(1)}, s32[]{:S(2)}) async-start(s8[16384000]{0:T(1024)(128)(4,1)} %bitcast.75), calls=%async_computation.10 | async-start | bytes 8388608
  390.8 9.9 %slice-start.3 = ((s8[16384000]{0:T(1024)(128)(4,1)}), s8[3801088]{0:T(1024)(128)(4,1)S(1)}, s32[]{:S(2)}) async-start(s8[16384000]{0:T(1024)(128)(4,1)} %bitcast.75), calls=%async_computation.11 | async-start | bytes 7602176
  411.2 2.6 copy-start.10
  413.9 7.6 %copy-start.9 = (f32[3200]{0:T(1024)S(1)}, f32[3200]{0:T(1024)}, u32[]{:S(2)}) copy-start(f32[3200]{0:T(1024)} %param.33) | copy-start | bytes 38404
  572.1 5.7 copy-start.1
  572.1 5.7 copy-start.5
  572.1 7.4 %slice-start.6 = ((s8[8192000]{0:T(1024)(128)(4,1)}), s8[4194304]{0:T(1024)(128)(4,1)S(1)}, s32[]{:S(2)}) async-start(s8[8192000]{0:T(1024)(128)(4,1)} %bitcast.81), calls=%async_computation.14 | async-start | bytes 8388608
  577.8 2.6 slice-start.7
  577.8 2.6 copy-start.4
  580.4 1.7 copy-start.6
Sparse Core Ops, SparseCore 0:
  85.8 46.4 all-reduce.1
  584.9 23.8 reduce-scatter.1
Sparse Core Ops, SparseCore 1:
  87.8 147.4 all-gather.4
  236.7 145.9 all-gather.6
  384.1 145.9 all-gather.8
